TPU v7x, 32 devices: a whole 2x2x4 slice. The times are simulated.
32 devices in a mesh: prow: 4 (over y, x), pcol: 8 (over z, core).
Axes of the slice: x: 2, y: 2, z: 4, core: 2. Of those that a mesh axis runs over, the one named last changes fastest.
Arguments:
- matrix: float32 [16, 4, 256, 8, 8, 256], P(None, 'prow', None, None, 'pcol'), may hold values from -6 to 6, as said below
- factor: float32 [16, 4, 256, 8, 8, 256], P(None, 'prow', None, None, 'pcol'), may hold values from -3 to 3, as said below
Outputs:
- reduced: float32 [16, 4, 256, 8, 8, 256], P(None, 'prow', None, None, 'pcol')
Inputs may be any that keep to these rules, and one draw needn't show every extreme that they name: Symmetric matrix stored in its lower triangle: every entry above the diagonal is zero. `factor`: lower triangular with diagonal entries between 1 and 3; every entry above the diagonal is zero.
All inputs are finite; a program needn't handle non-finite values.
Results may differ from a plain program's by a relative error of at most 0.0001.
Values sent between devices are 32-bit elements; how exact they have to be, the bound alone decides.
A program may use at most 256 MiB of HBM per device.

v0:
```python
import jax
import jax.numpy as jnp
from jax import lax
from jax.sharding import PartitionSpec as P

BLOCKS = 2
BASE = 16

highest = lax.Precision.HIGHEST
high = lax.Precision.HIGH


def product(left, right):
    return jnp.dot(left, right, precision=highest, preferred_element_type=jnp.float32)


def product_trans(left, right, precision=highest):
    return lax.dot_general(
        left, right, (((1,), (1,)), ((), ())), precision=precision, preferred_element_type=jnp.float32
    )


def batched(left, right):
    return jnp.einsum("bij,bjk->bik", left, right, precision=highest, preferred_element_type=jnp.float32)


def invert(lower):
    count, width, _ = lower.shape
    size = BASE if width % BASE == 0 else width

    def blocks(extent, row, col):
        return lower[:, row * extent : (row + 1) * extent, col * extent : (col + 1) * extent]

    parts = width // size
    diag = jnp.stack([blocks(size, i, i) for i in range(parts)], 1).reshape(count * parts, size, size)
    rows = jnp.arange(size)[None, :, None]
    result = jnp.broadcast_to(jnp.eye(size, dtype=jnp.float32), diag.shape)
    for i in range(size):
        pivot = result[:, i : i + 1, :] / diag[:, i : i + 1, i : i + 1]
        changed = jnp.where(rows > i, result - diag[:, :, i : i + 1] * pivot, result)
        result = lax.optimization_barrier(jnp.where(rows == i, pivot, changed))
    while parts > 1:
        pairs = parts // 2
        split = result.reshape(count * pairs, 2, size, size)
        upper, under = split[:, 0], split[:, 1]
        cross = jnp.stack([blocks(size, 2 * j + 1, 2 * j) for j in range(pairs)], 1)
        cross = cross.reshape(count * pairs, size, size)
        corner = -batched(batched(under, cross), upper)
        top = jnp.concatenate([upper, jnp.zeros_like(upper)], 2)
        result = jnp.concatenate([top, jnp.concatenate([corner, under], 2)], 1)
        parts, size = pairs, 2 * size
    return result.reshape(count, width, width)


def core_of(block, inverse):
    symmetric = block + block.T - jnp.diag(jnp.diagonal(block))
    inner = product_trans(product(inverse, symmetric), inverse)
    return 0.5 * (inner + inner.T)


def on_device(matrix, factor):
    row_tiles = matrix.shape[0]
    width = matrix.shape[2]
    col_tiles = matrix.shape[3]
    prow_count = lax.axis_size("prow")
    pcol_count = lax.axis_size("pcol")
    prow_index = lax.axis_index("prow")
    pcol_index = lax.axis_index("pcol")
    height = row_tiles * width
    breadth = col_tiles * width
    tile_rows = jnp.arange(row_tiles, dtype=jnp.int32) * prow_count + prow_index
    tile_cols = jnp.arange(col_tiles, dtype=jnp.int32) * pcol_count + pcol_index
    offsets = jnp.arange(width, dtype=jnp.int32)
    elem_rows = (tile_rows[:, None] * width + offsets[None, :]).reshape(height)
    elem_cols = (tile_cols[:, None] * width + offsets[None, :]).reshape(breadth)
    row_tile_of = jnp.repeat(tile_rows, width)[:, None]
    col_tile_of = jnp.repeat(tile_cols, width)[:, None]
    ratio = pcol_count // prow_count
    keeper = prow_index == pcol_index % prow_count

    raw = []
    for step in range(BLOCKS):
        place = step // pcol_count
        raw.append((matrix[:, 0, :, place, 0, :], factor[:, 0, :, place, 0, :]))

    wanted = []
    for tile in range(BLOCKS):
        for step in range(tile + 1):
            held = (prow_index == tile % prow_count) & (pcol_index == step % pcol_count)
            for source in raw[step]:
                wanted.append(jnp.where(held, source[tile // prow_count], 0.0))
    corners = lax.psum(jnp.stack(wanted), ("prow", "pcol"))
    corner = {}
    index = 0
    for tile in range(BLOCKS):
        for step in range(tile + 1):
            corner[tile, step] = (corners[index], corners[index + 1])
            index += 2

    def select_columns(panel):
        shaped = panel.reshape(col_tiles, ratio, width, width)
        return lax.dynamic_index_in_dim(shaped, pcol_index // prow_count, 1, keepdims=False)

    row_panels, col_panels = [], []
    for step in range(BLOCKS):
        owner = pcol_index == step % pcol_count
        got = lax.psum(tuple(jnp.where(owner, source, 0.0) for source in raw[step]), "pcol")
        row_panels.append(tuple(part.reshape(height, width) for part in got))
        picked = lax.psum(tuple(jnp.where(keeper, select_columns(part), 0.0) for part in got), "prow")
        col_panels.append(tuple(part.reshape(breadth, width) for part in picked))

    inverses = invert(jnp.stack([corner[step, step][1] for step in range(BLOCKS)]))

    cores = []
    tile_half = {}
    for step in range(BLOCKS):
        block = corner[step, step][0]
        for before in range(step):
            half, fact = tile_half[step, before]
            block = block - jnp.tril(product_trans(half, fact) + product_trans(fact, half))
        inverse = inverses[step]
        core = core_of(block, inverse)
        cores.append(core)
        for tile in range(step + 1, BLOCKS):
            piece, fact = corner[tile, step]
            for before in range(step):
                half_row, fact_row = tile_half[tile, before]
                half_col, fact_col = tile_half[step, before]
                piece = piece - product_trans(half_row, fact_col) - product_trans(fact_row, half_col)
            tile_half[tile, step] = (product_trans(piece, inverse) - 0.5 * product(fact, core), fact)

    def reduce_panels(panels, tile_of):
        halves, facts, finals = [], [], []
        for step in range(BLOCKS):
            panel, fact = panels[step]
            below = tile_of > step
            fact = jnp.where(below, fact, 0.0)
            for before in range(step):
                half_col, fact_col = tile_half[step, before]
                panel = panel - product_trans(
                    jnp.concatenate([halves[before], facts[before]], 1),
                    jnp.concatenate([fact_col, half_col], 1),
                )
            shared = product(fact, cores[step])
            half = jnp.where(below, product_trans(panel, inverses[step]), 0.0) - 0.5 * shared
            halves.append(half)
            facts.append(fact)
            finals.append(half - 0.5 * shared)
        return halves, facts, finals

    row_half, row_fact, finals = reduce_panels(row_panels, row_tile_of)
    col_half, col_fact, _ = reduce_panels(col_panels, col_tile_of)
    left = jnp.concatenate([part for pair in zip(row_half, row_fact) for part in pair], 1)
    right = jnp.concatenate([part for pair in zip(col_fact, col_half) for part in pair], 1)
    update = product_trans(left, right, high)
    local = matrix.reshape(height, breadth)
    local = local - jnp.where(elem_rows[:, None] >= elem_cols[None, :], update, 0.0)
    for step in range(BLOCKS):
        first = step // pcol_count * width
        current = local[:, first : first + width]
        diag_rows = jnp.tile(jnp.tril(cores[step]), (row_tiles, 1))
        column = jnp.where(row_tile_of == step, diag_rows, jnp.where(row_tile_of > step, finals[step], current))
        column = jnp.where(pcol_index == step % pcol_count, column, current)
        local = local.at[:, first : first + width].set(column)
    return local.reshape(row_tiles, 1, width, col_tiles, 1, width)


def solution(mesh):
    placed = P(None, "prow", None, None, "pcol", None)
    return jax.shard_map(on_device, mesh=mesh, in_specs=(placed, placed), out_specs=placed, check_vma=False)
```

profile of v0, /device:TPU:25, one launch (start us, length us, event | category | flops | bytes accessed | tf_op | source)
XLA Modules:
  0.0 876.0 jit_solution(8016696733492530095)
XLA Ops:
  10.3 12.9 %broadcast_select_fusion.2 = (f32[16,1,256,1,1,256]{5,4,3,2,1,0:T(1,128)S(1)}, f32[16,1,256,1,1,256]{5,4,3,2,1,0:T(1,128)S(1)}, f32[16,1,256,1,1,256]{5,4,3,2,1,0:T(1,128)S(1)}, f32[16,1,256,1,1,256]{5,4,3,2,1,0:T(1,128)S(1)}) fusion(pred[]{:T(512)S(6)} %eq.189, f32[16,1,256,8,1,256]{5,4,3,2,1,0:T(1,128)} %param.7, pred[]{:T(512)S(6)} %eq.209, ...), kind=kLoop, calls=%fused_computation.23 | loop fusion | flops 4194304 | bytes 25165826 | tf_op jit(solution)/shard_map/jit(_where)/select_n | solution.py:107
  23.1 2.5 copy.139
  25.6 2.4 copy.140
  28.0 2.5 copy.141
  30.5 2.4 copy.142
  34.1 94.7 %reduce.9 = f32[16,256,8,256]{3,2,1,0:T(8,128)} reduce(f32[16,1,256,8,1,256]{5,4,3,2,1,0:T(1,128)} %param.6, f32[]{:T(128)} %constant.197), dimensions={1,4}, to_apply=%param.6.reduce_sub_computation | reduce | bytes 67108864 | tf_op args[0]
  128.8 30.0 %copy.119 = f32[512,8,8,256]{3,1,2,0:T(8,128)} copy(f32[512,8,8,256]{3,2,1,0:T(8,128)} %bitcast.373) | data formatting | bytes 67108864
  158.8 31.2 %copy.96 = f32[4096,2048]{0,1:T(8,128)} copy(f32[4096,2048]{1,0:T(8,128)} %bitcast.374) | data formatting | bytes 67108864 | tf_op jit(solution)/shard_map/reshape | solution.py:156
  193.7 2.0 slice_bitcast_fusion.4
  205.1 274.9 %all-reduce.12.cloned.1.call-done = (f32[16,256,256]{2,1,0:T(8,128)}, f32[16,256,256]{2,1,0:T(8,128)}, f32[16,256,256]{2,1,0:T(8,128)}, f32[16,256,256]{2,1,0:T(8,128)}) async-done(((f32[16,256,256]{2,1,0:T(8,128)}, f32[16,256,256]{2,1,0:T(8,128)}, f32[16,256,256]{2,1,0:T(8,128)}, f32[16,256,256]{2,1,0:T(8,128)}), (f32[16,256,256]{2,1,0:T(8,128)}, f32[16,256,256]{2,1,0:T(8,128)}, f32[16,256,256]{2,1,0:T(8,128)}, ...) | async-done | bytes 16777232 | tf_op jit(solution)/shard_map/psum | solution.py:107
  480.0 3.1 constant_dynamic-slice_fusion
  483.1 2.4 copy.117
  485.7 2.2 copy.125
  488.2 1.5 constant_dynamic-slice_fusion.3
  489.6 2.2 copy.114
  492.0 2.3 copy.122
  494.5 1.5 constant_dynamic-slice_fusion.2
  496.0 2.2 copy.115
  498.4 2.2 copy.123
  500.9 1.5 constant_dynamic-slice_fusion.1
  502.4 2.2 copy.116
  504.7 2.2 copy.124
  508.4 2.4 gather_fusion
  514.5 2.7 gather_fusion.1
  518.9 5.7 copy.126
  525.1 5.9 copy.127
  531.0 5.9 copy.98
  536.9 6.0 copy.97
  542.9 3.0 broadcast_select_fusion.5
  545.9 4.3 convolution_multiply_fusion.1
  550.7 4.3 convolution_multiply_fusion
  555.4 5.1 fusion.18
  560.5 14.3 %fusion.20 = f32[4096,256]{1,0:T(8,128)S(1)} fusion(f32[4096,256]{1,0:T(8,128)S(1)} %bitcast.395, f32[4096,256]{0,1:T(8,128)S(1)} %broadcast_select_fusion.5, f32[4096,256]{0,1:T(8,128)S(1)} %fusion.18, f32[256,256]{1,0:T(8,128)S(1)} %fusion.34, f32[256,256]{1,0:T(8,128)S(1)} %get-tuple-element.45), kind=kOutput, calls=%fused_computation.33 | convolution fusion | flops 6445727744 | bytes 17301504 | tf_op jit(solution)/shard_map/dot_general | solution.py:18
  574.9 5.9 fusion.19
  580.8 99.2 %all-reduce.14.cloned.1.call-done = (f32[2048,256]{0,1:T(8,128)}, f32[2048,256]{0,1:T(8,128)}, f32[2048,256]{0,1:T(8,128)}, f32[2048,256]{0,1:T(8,128)}) async-done(((f32[2048,256]{0,1:T(8,128)}, f32[2048,256]{0,1:T(8,128)}, f32[2048,256]{0,1:T(8,128)}, f32[2048,256]{0,1:T(8,128)}), (f32[2048,256]{0,1:T(8,128)}, f32[2048,256]{0,1:T(8,128)}, f32[2048,256]{0,1:T(8,128)}, ...) | async-done | bytes 8388624 | tf_op jit(solution)/shard_map/psum | solution.py:109
  680.0 2.0 broadcast_select_fusion.7
  682.2 2.0 convolution_select_fusion.3
  684.3 2.2 fusion.32
  686.4 3.9 fusion.28
  690.4 2.0 convolution_select_fusion.2
  692.6 2.4 fusion.31
  695.1 4.7 fusion.122
  699.8 1.6 copy-done.6
  701.4 66.9 %select_subtract_fusion = f32[4096,2048]{0,1:T(8,128)} fusion(f32[4096,2048]{0,1:T(8,128)} %copy.96, f32[4096,256]{0,1:T(8,128)} %copy-done.7, f32[4096,256]{0,1:T(8,128)} %fusion.19, f32[4096,256]{0,1:T(8,128)S(1)} %copy-done.4, f32[4096,256]{0,1:T(8,128)S(1)} %copy-done.6, s32[4096]{0:T(1024)S(1)} %bitcast.452, s32[2048]{0:T(1024)S(1)} %bitcast.453, ...), kind=kOutput, calls=%fused_computation.2 | convolution fusion | flops 51577356288 | bytes 92299264 | tf_op jit(solution)/shard_map/dot_general | solution.py:18
  768.4 13.0 %constant_dynamic-update-slice_fusion.24 = (f32[4096,2048]{0,1:T(8,128)}, f32[4096,256]{0,1:T(8,128)}) fusion(f32[4096,2048]{0,1:T(8,128)} %select_subtract_fusion, f32[4096,256]{0,1:T(8,128)} %bitcast.386, f32[4096,256]{0,1:T(8,128)} %copy-done.5, f32[4096,256]{0,1:T(8,128)} %copy-done.2, pred[4096]{0:T(1024)(128)(4,1)S(1)} %gt.185, ...), kind=kLoop, calls=%fused_computation.230 | loop fusion | flops 5242880 | bytes 25174528 | tf_op jit(solution)/shard_map/scatter | solution.py:164
  781.4 9.0 %fusion.23 = f32[4096,2048]{0,1:T(8,128)} fusion(f32[4096,2048]{0,1:T(8,128)} %get-tuple-element.37, f32[4096,256]{0,1:T(8,128)} %get-tuple-element.38, f32[4096,256]{0,1:T(8,128)} %bitcast.379, f32[4096,256]{0,1:T(8,128)} %fusion.19, f32[4096,256]{0,1:T(8,128)S(1)} %copy-done.1, pred[4096]{0:T(1024)(128)(4,1)S(1)} %copy-done.23, pred[]{:T(512)S(6)} %eq.209, ...), kind=kLoop, calls=%fused_computation.34 | loop fusion | flops 5242880 | bytes 20980224 | tf_op jit(solution)/shard_map/scatter | solution.py:164
  790.4 30.2 %copy.128 = f32[256,8,16,256]{3,2,1,0:T(8,128)} copy(f32[256,8,16,256]{3,1,2,0:T(8,128)} %bitcast.378) | data formatting | bytes 67108864
  820.5 48.7 %copy.92 = f32[16,1,256,8,1,256]{5,4,3,2,1,0:T(1,128)} copy(f32[16,1,256,8,1,256]{2,0,5,3,4,1:T(8,128)} %bitcast.375) | data formatting | bytes 67108864 | tf_op jit(solution)/shard_map/reshape | solution.py:165
  (226 shorter events, 27.0 us)
Async XLA Ops:
  6.5 187.2 %all-reduce.10.cloned.1.call-start = ((), (), s32[]{:S(2)}) async-start(), calls=%async_computation | async-start | bytes 3145728 | tf_op jit(solution)/shard_map/psum | solution.py:92
  9.0 1.1 copy-start.15
  10.2 469.8 %all-reduce.12.cloned.1.call-start = ((), (), s32[]{:S(2)}) async-start(), calls=%async_computation.1 | async-start | bytes 33554432 | tf_op jit(solution)/shard_map/psum | solution.py:107
  32.9 647.0 %all-reduce.14.cloned.1.call-start = ((), (), s32[]{:S(2)}) async-start(), calls=%async_computation.2 | async-start | bytes 16777216 | tf_op jit(solution)/shard_map/psum | solution.py:109
  485.5 2.7 copy-start.11
  491.9 2.7 copy-start.9
  498.2 2.7 copy-start.12
  506.9 0.9 copy-start.20
  506.9 1.0 copy-start.21
  506.9 1.3 copy-start.19
  507.0 4.5 copy-start.14
  545.9 14.6 %copy-start.3 = (f32[4096,256]{0,1:T(8,128)}, f32[4096,256]{0,1:T(8,128)S(1)}, u32[]{:S(2)}) copy-start(f32[4096,256]{0,1:T(8,128)S(1)} %broadcast_select_fusion.5) | copy-start | bytes 12582916
  545.9 4.3 copy-start.8
  550.2 4.9 copy-start.2
  550.7 4.4 copy-start.7
  550.7 4.7 copy-start.10
  555.0 19.8 %copy-start = (f32[4096,256]{0,1:T(8,128)}, f32[4096,256]{0,1:T(8,128)S(1)}, u32[]{:S(2)}) copy-start(f32[4096,256]{0,1:T(8,128)S(1)} %convolution_multiply_fusion) | copy-start | bytes 12582916
  555.4 5.1 copy-start.13
  560.5 14.4 %copy-start.5 = (f32[4096,256]{0,1:T(8,128)}, f32[4096,256]{0,1:T(8,128)S(1)}, u32[]{:S(2)}) copy-start(f32[4096,256]{0,1:T(8,128)S(1)} %fusion.18) | copy-start | bytes 12582916
  574.9 105.1 %copy-start.22 = (pred[2048]{0:T(1024)(128)(4,1)S(1)}, pred[2048]{0:T(1024)(128)(4,1)}, u32[]{:S(2)}) copy-start(pred[2048]{0:T(1024)(128)(4,1)} %gt.206) | copy-start | bytes 6148
  680.0 2.2 copy-start.17
  684.2 2.2 copy-start.16
  690.4 2.1 copy-start.18
  695.0 4.8 copy-start.4
  695.0 6.4 copy-start.6
  695.0 6.4 copy-start.25
  695.1 6.4 copy-start.26
  701.4 67.0 %copy-start.24 = (pred[4096]{0:T(1024)(128)(4,1)S(1)}, pred[4096]{0:T(1024)(128)(4,1)}, u32[]{:S(2)}) copy-start(pred[4096]{0:T(1024)(128)(4,1)} %eq.213) | copy-start | bytes 12292
  768.4 13.0 %copy-start.1 = (f32[4096,256]{0,1:T(8,128)S(1)}, f32[4096,256]{0,1:T(8,128)}, u32[]{:S(2)}) copy-start(f32[4096,256]{0,1:T(8,128)} %copy-done) | copy-start | bytes 12582916
  768.4 13.0 %copy-start.23 = (pred[4096]{0:T(1024)(128)(4,1)S(1)}, pred[4096]{0:T(1024)(128)(4,1)}, u32[]{:S(2)}) copy-start(pred[4096]{0:T(1024)(128)(4,1)} %eq.215) | copy-start | bytes 12292
Sparse Core Ops, SparseCore 0:
  12.6 130.6 all-reduce.9
  146.2 333.8 all-reduce.11
  507.1 172.8 all-reduce.13
where the time goes:
time: 884 us; the launch traced here: 876 us
  waiting for transfers between devices  374 us (42%)
  local copies, waits for them, and re-layouts  220 us (25%)
  other arithmetic  147 us (17%)
  matrix products  119 us (13%)
  between operations  14.7 us (2%)
    psum x1, waiting for transfers between devices, on_device(): lax.psum(tuple((jnp.where(owner, source, 0.0) for source in raw[step])),...  275 us
    unnamed x75, local copies, waits for them, and re-layouts  106 us
    dot_general x12, matrix products, product_trans(): lax.dot_general(left, right, (((1,), (1,)), ((), ())), precision=precisio...  102 us
    psum x1, waiting for transfers between devices, on_device(): lax.psum(tuple((jnp.where(keeper, select_columns(part), 0.0) for part in...  99.2 us
    unnamed x23, other arithmetic  95.9 us
    reshape x1, local copies, waits for them, and re-layouts, on_device(): return local.reshape(row_tiles, 1, width, col_tiles, 1, width)  48.7 us
    reshape x1, local copies, waits for them, and re-layouts, on_device(): local = matrix.reshape(height, breadth)  31.2 us
    scatter x2, other arithmetic, on_device(): local = local.at[:, first:first + width].set(column)  22 us
  transfers between devices with their start and end apart: 3, of which 2 were waited for; matrix products, arithmetic and copies ran while one was open for 30% of the time, Pallas kernels for 0%

commit v1 on v0

v1 whole, which is shorter than its diff:
```python
import functools

import jax
import jax.numpy as jnp
from jax import lax
from jax.experimental import pallas as pl
from jax.experimental.pallas import tpu as pltpu
from jax.sharding import PartitionSpec as P

MESH = pl.DeviceIdType.MESH
CORES = 2
LAG = 2
LIMIT = 60 * 1024 * 1024

highest = lax.Precision.HIGHEST


def dot(left, right):
    return jnp.dot(left, right, precision=highest, preferred_element_type=jnp.float32)


def dot_trans(left, right, precision=highest):
    return lax.dot_general(
        left, right, (((1,), (1,)), ((), ())), precision=precision, preferred_element_type=jnp.float32
    )


def grid_of(count):
    across = 1
    while across * across * 4 <= count:
        across *= 2
    return count // across, across


def gather_kernel(
    prows, pcols, matrix, factor, row_out, col_out, fin_out,
    rows, cols, panel, corner, inverse, core, half,
    load_sem, row_recv, col_recv, corner_recv, corner_send,
    down_send, side_send, col_send, relay_send, out_sem,
):
    row_tiles, _, width, _ = rows.shape
    col_tiles = cols.shape[0]
    high, across = grid_of(prows)
    depth = pcols // CORES
    ratio = pcols // prows
    prow = lax.axis_index("prow")
    pcol = lax.axis_index("pcol")
    plane = pcol // CORES
    side = pcol % CORES
    y, x = prow // across, prow % across
    top = plane == 0

    barrier = pltpu.get_barrier_semaphore()

    def greet(where):
        pl.semaphore_signal(barrier, inc=1, device_id=where, device_id_type=MESH)

    def greet_plane(index, _):
        other = (index // CORES, plane * CORES + index % CORES)

        @pl.when(index != prow * CORES + side)
        def _():
            greet(other)

        return 0

    lax.fori_loop(0, prows * CORES, greet_plane, 0)

    @pl.when(plane > 0)
    def _():
        greet((prow, pcol - CORES))

    @pl.when(plane < depth - 1)
    def _():
        greet((prow, pcol + CORES))

    greeted = prows * CORES - 1 + jnp.where(plane > 0, 1, 0) + jnp.where(plane < depth - 1, 1, 0)
    pl.semaphore_wait(barrier, greeted)

    def remote(source, target, send, recv, where):
        return pltpu.make_async_remote_copy(
            src_ref=source, dst_ref=target, send_sem=send, recv_sem=recv, device_id=where, device_id_type=MESH
        )

    def down_copy(i, late):
        kind = side + CORES * late
        return remote(
            rows.at[i, kind], rows.at[i, kind], down_send.at[i, late], row_recv.at[i, kind], (prow, pcol + CORES)
        )

    def side_copy(i, late, kind):
        return remote(
            rows.at[i, kind], rows.at[i, kind], side_send.at[i, late], row_recv.at[i, kind],
            (prow, plane * CORES + 1 - side),
        )

    def ways(source):
        ys, xs = source // across, source % across
        return (
            ((x == xs) & (y >= ys) & (y + 1 < high), prow + across),
            ((x == xs) & (y <= ys) & (y >= 1), prow - across),
            ((x >= xs) & (x + 1 < across), prow + 1),
            ((x <= xs) & (x >= 1), prow - 1),
        )

    def for_columns(i, late, act):
        kind = side + CORES * late
        for other in range(CORES):
            column = plane * CORES + other
            first = column // prows
            j = (i - first) // ratio

            @pl.when((column % prows == prow) & (i >= first) & ((i - first) % ratio == 0))
            def _():
                for way, (fits, where) in enumerate(ways(prow)):
                    @pl.when(fits)
                    def _():
                        act(remote(
                            rows.at[i, kind], cols.at[j, kind], col_send.at[other, way, i, late],
                            col_recv.at[j, kind], (where, column),
                        ))

    def emit(i, late):
        @pl.when(plane < depth - 1)
        def _():
            down_copy(i, late).start()

        side_copy(i, late, side + CORES * late).start()
        for_columns(i, late, lambda copy: copy.start())

    source = pcol % prows
    first_tile = pcol // prows

    def for_relay(i, late, act):
        j = (i - first_tile) // ratio

        @pl.when((prow != source) & (i >= first_tile) & ((i - first_tile) % ratio == 0))
        def _():
            for kind in (CORES * late, CORES * late + 1):
                act(j, kind)

    def relay_copies(j, kind, act):
        for way, (fits, where) in enumerate(ways(source)):
            @pl.when(fits)
            def _():
                act(remote(
                    cols.at[j, kind], cols.at[j, kind], relay_send.at[way, j, kind], col_recv.at[j, kind],
                    (where, pcol),
                ))

    def arrive_column(j, kind):
        remote(
            cols.at[j, kind], cols.at[j, kind], relay_send.at[0, j, kind], col_recv.at[j, kind], (prow, pcol)
        ).wait_recv()
        relay_copies(j, kind, lambda copy: copy.start())

    def relay(i, late):
        for_relay(i, late, arrive_column)

    def load(which, i):
        if which == 0:
            return pltpu.make_async_copy(factor.at[i, 0, :, 0, 0, :], rows.at[i, side], load_sem.at[0, i])
        return pltpu.make_async_copy(matrix.at[i, 0, :, 0, 0, :], panel.at[i], load_sem.at[1, i])

    owner = top & (prow < 2) & (side <= prow)
    slot = 2 * (prow + side)

    def corner_copy(which, index):
        sent = panel.at[0] if which == 0 else rows.at[0, side]
        return remote(
            sent, corner.at[slot + which], corner_send.at[which, index], corner_recv.at[slot + which],
            (index // CORES, index % CORES),
        )

    def each_peer(act):
        def body(index, _):
            @pl.when(index != prow * CORES + side)
            def _():
                for which in range(2):
                    act(corner_copy(which, index))
            return 0
        lax.fori_loop(0, prows * CORES, body, 0)

    row_id = lax.broadcasted_iota(jnp.int32, (width, width), 0)
    col_id = lax.broadcasted_iota(jnp.int32, (width, width), 1)

    @pl.when(top)
    def _():
        def start_loads(i, _):
            load(1, i).start()
            load(0, i).start()
            return 0
        lax.fori_loop(0, row_tiles, start_loads, 0)
        load(1, 0).wait()
        load(0, 0).wait()

        @pl.when(owner)
        def _():
            each_peer(lambda copy: copy.start())
            corner[slot] = panel[0]
            corner[slot + 1] = rows[0, side]

        emit(0, 0)

        def send_early(i, _):
            load(0, i).wait()
            emit(i, 0)
            return 0
        lax.fori_loop(1, row_tiles, send_early, 0)

        def await_corner(index, _):
            @pl.when(jnp.logical_not(owner & ((index == slot) | (index == slot + 1))))
            def _():
                remote(
                    corner.at[index], corner.at[index], corner_send.at[0, 0], corner_recv.at[index], (prow, pcol)
                ).wait_recv()
            return 0
        lax.fori_loop(0, 6, await_corner, 0)

        levels = (width - 1).bit_length()

        def invert(step, _):
            lower = corner[1 + 4 * step]
            diagonal = row_id == col_id
            inverse[step] = jnp.where(diagonal, 1.0 / jnp.where(diagonal, lower, 1.0), 0.0)

            def level(bit, _):
                block = lax.shift_right_logical(row_id, bit)
                under = (block % 2 == 1) & (lax.shift_right_logical(col_id, bit) == block - 1)
                now = inverse[step]
                cross = jnp.where(under, corner[1 + 4 * step], 0.0)
                inverse[step] = now - dot(dot(now, cross), now)
                return 0
            lax.fori_loop(0, levels, level, 0)
            return 0
        lax.fori_loop(0, 2, invert, 0)

        def core_of(block, inv):
            symmetric = block + block.T - jnp.where(row_id == col_id, block, 0.0)
            inner = dot_trans(dot(inv, symmetric), inv)
            return 0.5 * (inner + inner.T)

        core[0] = core_of(corner[0], inverse[0])
        half[...] = dot_trans(corner[2], inverse[0]) - 0.5 * dot(corner[3], core[0])
        cross = dot_trans(half[...], corner[3]) + dot_trans(corner[3], half[...])
        corner[4] = corner[4] - jnp.where(row_id >= col_id, cross, 0.0)
        core[1] = core_of(corner[4], inverse[1])

        @pl.when(owner)
        def _():
            each_peer(lambda copy: copy.wait_send())

    @pl.when(jnp.logical_not(top))
    def _():
        def pass_early(i, _):
            down_copy(i, 0).wait_recv()
            emit(i, 0)
            relay(i - LAG, 0)
            return 0
        lax.fori_loop(0, row_tiles, pass_early, 0)

    def reduce_tile(i):
        @pl.when(i > 0)
        def _():
            load(1, i).wait()

        @pl.when(side == 1)
        def _():
            for late in range(2):
                side_copy(i, late, 2 * late).wait_recv()
            panel[i] = (
                panel[i] - dot_trans(rows[i, 2], corner[3]) - dot_trans(rows[i, 0], half[...])
            )

        shared = dot(rows[i, side], core[side])
        halfway = dot_trans(panel[i], inverse[side]) - 0.5 * shared
        rows[i, side + 2] = halfway
        tile = i * prows + prow
        lower = jnp.where(row_id >= col_id, core[side], 0.0)
        final = halfway - 0.5 * shared
        final = jnp.where(tile > side, final, jnp.where(tile == side, lower, 0.0))
        panel[i] = final

    def late_step(i, _):
        @pl.when(top & (i < row_tiles))
        def _():
            reduce_tile(i)

        @pl.when(i >= 1)
        def _():
            @pl.when(jnp.logical_not(top))
            def _():
                down_copy(i - 1, 1).wait_recv()
            emit(i - 1, 1)

        @pl.when(top & (i < row_tiles))
        def _():
            relay(i, 0)

        @pl.when(jnp.logical_not(top) & (i < LAG))
        def _():
            relay(row_tiles - LAG + i, 0)

        relay(i - 1 - LAG, 1)
        return 0
    lax.fori_loop(0, row_tiles + 1, late_step, 0)
    for back in range(LAG):
        relay(row_tiles - LAG + back, 1)

    def await_side(i, _):
        @pl.when(jnp.logical_not(top & (side == 1)))
        def _():
            for late in range(2):
                side_copy(i, late, 1 - side + 2 * late).wait_recv()
        return 0
    lax.fori_loop(0, row_tiles, await_side, 0)

    outs = (
        pltpu.make_async_copy(rows, row_out, out_sem.at[0]),
        pltpu.make_async_copy(cols, col_out, out_sem.at[1]),
        pltpu.make_async_copy(panel, fin_out, out_sem.at[2]),
    )
    outs[0].start()

    @pl.when(prow != source)
    def _():
        outs[1].start()

    @pl.when(top)
    def _():
        outs[2].start()

    def drain(i, _):
        for late in range(2):
            @pl.when(plane < depth - 1)
            def _():
                down_copy(i, late).wait_send()
            side_copy(i, late, side + 2 * late).wait_send()
            for_columns(i, late, lambda copy: copy.wait_send())
            for_relay(i, late, lambda j, kind: relay_copies(j, kind, lambda copy: copy.wait_send()))
        return 0
    lax.fori_loop(0, row_tiles, drain, 0)

    outs[0].wait()

    @pl.when(prow != source)
    def _():
        outs[1].wait()

    @pl.when(top)
    def _():
        outs[2].wait()


def split(value):
    high = value.astype(jnp.bfloat16)
    return high, (value - high.astype(jnp.float32)).astype(jnp.bfloat16)


def update_kernel(
    prows, pcols, matrix, row_in, col_in, fin_in, out,
    rows, row_high, row_low, staged, col_high, col_low, tiles, zeros,
    row_sem, col_sem, in_sem, out_sem,
):
    row_tiles = row_in.shape[0]
    col_tiles, _, width, _ = col_in.shape
    ratio = pcols // prows
    prow = lax.axis_index("prow")
    pcol = lax.axis_index("pcol")
    source = pcol % prows
    first_tile = pcol // prows
    fixed = pcol < 2
    row_id = lax.broadcasted_iota(jnp.int32, (width, width), 0)
    col_id = lax.broadcasted_iota(jnp.int32, (width, width), 1)
    zeros[...] = jnp.zeros_like(zeros)

    def row_copy(i):
        return pltpu.make_async_copy(row_in.at[i], rows.at[i % 2], row_sem.at[i % 2])

    def col_start(j):
        @pl.when(prow == source)
        def _():
            pltpu.make_async_copy(row_in.at[ratio * j + first_tile], staged.at[j % 2], col_sem.at[j % 2]).start()

        @pl.when(prow != source)
        def _():
            pltpu.make_async_copy(col_in.at[j], staged.at[j % 2], col_sem.at[j % 2]).start()

    def live(i, j):
        return j * pcols + pcol <= i * prows + prow

    def is_fixed(j):
        return fixed & (j == 0)

    def start_loads(i):
        def body(j, _):
            @pl.when(live(i, j) & jnp.logical_not(is_fixed(j)))
            def _():
                pltpu.make_async_copy(matrix.at[i, 0, :, j, 0, :], tiles.at[i % 3, j], in_sem.at[i % 3, j]).start()

            @pl.when(live(i, j) & is_fixed(j))
            def _():
                pltpu.make_async_copy(fin_in.at[i], tiles.at[i % 3, j], in_sem.at[i % 3, j]).start()
            return 0
        lax.fori_loop(0, col_tiles, body, 0)

    def out_copy(i, j):
        return pltpu.make_async_copy(tiles.at[i % 3, j], out.at[i, 0, :, j, 0, :], out_sem.at[i % 3, j])

    def zero_copy(i, j):
        return pltpu.make_async_copy(zeros, out.at[i, 0, :, j, 0, :], out_sem.at[i % 3, j])

    def wait_outs(i):
        def body(j, _):
            out_copy(i, j).wait()
            return 0
        lax.fori_loop(0, col_tiles, body, 0)

    col_start(0)
    row_copy(0).start()
    start_loads(0)

    def prepare(j, _):
        @pl.when(j + 1 < col_tiles)
        def _():
            col_start(j + 1)
        pltpu.make_async_copy(col_in.at[j], staged.at[j % 2], col_sem.at[j % 2]).wait()
        for kind in range(4):
            upper, lower = split(staged[j % 2, kind])
            place = pl.ds((kind + 2) % 4 * width, width)
            col_high[j, :, place] = upper
            col_low[j, :, place] = lower
        return 0
    lax.fori_loop(0, col_tiles, prepare, 0)

    def row_step(i, _):
        @pl.when(i >= 2)
        def _():
            wait_outs(i - 2)

        @pl.when(i + 1 < row_tiles)
        def _():
            row_copy(i + 1).start()
            start_loads(i + 1)
        row_copy(i).wait()
        for kind in range(4):
            upper, lower = split(rows[i % 2, kind])
            row_high[:, kind * width:(kind + 1) * width] = upper
            row_low[:, kind * width:(kind + 1) * width] = lower

        def tile_step(j, _):
            @pl.when(live(i, j))
            def _():
                pltpu.make_async_copy(zeros, tiles.at[i % 3, j], in_sem.at[i % 3, j]).wait()

                @pl.when(jnp.logical_not(is_fixed(j)))
                def _():
                    total = (
                        dot_trans(row_high[...], col_low[j], None)
                        + dot_trans(row_low[...], col_high[j], None)
                        + dot_trans(row_high[...], col_high[j], None)
                    )
                    gap = ((i * prows + prow) - (j * pcols + pcol)) * width
                    tiles[i % 3, j] = tiles[i % 3, j] - jnp.where(row_id + gap >= col_id, total, 0.0)
                out_copy(i, j).start()

            @pl.when(jnp.logical_not(live(i, j)))
            def _():
                zero_copy(i, j).start()
            return 0
        lax.fori_loop(0, col_tiles, tile_step, 0)
        return 0
    lax.fori_loop(0, row_tiles, row_step, 0)
    for back in range(min(2, row_tiles), 0, -1):
        wait_outs(row_tiles - back)


def on_device(matrix, factor):
    row_tiles, _, width, col_tiles, _, _ = matrix.shape
    prows = lax.axis_size("prow")
    pcols = lax.axis_size("pcol")
    tile = (width, width)
    f32 = jnp.float32
    anywhere = pl.BlockSpec(memory_space=pl.ANY)
    dma = pltpu.SemaphoreType.DMA
    row_all, col_all, fin = pl.pallas_call(
        functools.partial(gather_kernel, prows, pcols),
        out_shape=(
            jax.ShapeDtypeStruct((row_tiles, 4) + tile, f32),
            jax.ShapeDtypeStruct((col_tiles, 4) + tile, f32),
            jax.ShapeDtypeStruct((row_tiles,) + tile, f32),
        ),
        in_specs=[anywhere, anywhere],
        out_specs=(anywhere, anywhere, anywhere),
        scratch_shapes=[
            pltpu.VMEM((row_tiles, 4) + tile, f32),
            pltpu.VMEM((col_tiles, 4) + tile, f32),
            pltpu.VMEM((row_tiles,) + tile, f32),
            pltpu.VMEM((6,) + tile, f32),
            pltpu.VMEM((2,) + tile, f32),
            pltpu.VMEM((2,) + tile, f32),
            pltpu.VMEM(tile, f32),
            dma((2, row_tiles)),
            dma((row_tiles, 4)),
            dma((col_tiles, 4)),
            dma((6,)),
            dma((2, prows * CORES)),
            dma((row_tiles, 2)),
            dma((row_tiles, 2)),
            dma((CORES, 4, row_tiles, 2)),
            dma((4, col_tiles, 4)),
            dma((3,)),
        ],
        compiler_params=pltpu.CompilerParams(collective_id=0, has_side_effects=True, vmem_limit_bytes=LIMIT),
        name="gather",
    )(matrix, factor)
    return pl.pallas_call(
        functools.partial(update_kernel, prows, pcols),
        out_shape=jax.ShapeDtypeStruct(matrix.shape, f32),
        in_specs=[anywhere] * 4,
        out_specs=anywhere,
        scratch_shapes=[
            pltpu.VMEM((2, 4) + tile, f32),
            pltpu.VMEM((width, 4 * width), jnp.bfloat16),
            pltpu.VMEM((width, 4 * width), jnp.bfloat16),
            pltpu.VMEM((2, 4) + tile, f32),
            pltpu.VMEM((col_tiles, width, 4 * width), jnp.bfloat16),
            pltpu.VMEM((col_tiles, width, 4 * width), jnp.bfloat16),
            pltpu.VMEM((3, col_tiles) + tile, f32),
            pltpu.VMEM(tile, f32),
            dma((2,)),
            dma((2,)),
            dma((3, col_tiles)),
            dma((3, col_tiles)),
        ],
        compiler_params=pltpu.CompilerParams(vmem_limit_bytes=LIMIT),
        name="update",
    )(matrix, row_all, col_all, fin)


def solution(mesh):
    placed = P(None, "prow", None, None, "pcol", None)
    return jax.shard_map(on_device, mesh=mesh, in_specs=(placed, placed), out_specs=placed, check_vma=False)
```

time: 884 us -> 282 us (0.32)
  waiting for transfers between devices: 374 us -> 0 us
  Pallas kernels: 0 us -> 282 us
  local copies, waits for them, and re-layouts: 220 us -> 0 us
  other arithmetic: 147 us -> 0 us
  matrix products: 119 us -> 0 us
  between operations: 14.7 us -> 0.01 us
    psum x3 -> x0, waiting for transfers between devices: 374 us -> none  [the longest x1 275 us: on_device(): lax.psum(tuple((jnp.where(owner, source, 0.0) for source in raw[step])),...]
    pallas_call x0 -> x2, Pallas kernels: none -> 282 us  [the longest x1 227 us: on_device(): pl.pallas_call(functools.partial(gather_kernel, prows, pcols), out_shape=...]
    dot_general x27 -> x0, matrix products: 119 us -> none  [the longest x12 102 us: product_trans(): lax.dot_general(left, right, (((1,), (1,)), ((), ())), precision=precisio...]
    unnamed x75 -> x0, local copies, waits for them, and re-layouts: 106 us -> none
    unnamed x23 -> x0, other arithmetic: 95.9 us -> none
    reshape x5 -> x0, local copies, waits for them, and re-layouts: 92 us -> none  [the longest x1 48.7 us: on_device(): return local.reshape(row_tiles, 1, width, col_tiles, 1, width)]
    scatter x2 -> x0, other arithmetic: 22 us -> none  [on_device(): local = local.at[:, first:first + width].set(column)]
    select_n x27 -> x0, other arithmetic: 21.5 us -> none  [the longest x1 12.9 us: on_device(): jnp.where(owner, source, 0.0)]
  transfers between devices with their start and end apart: 3 -> 0, of which waited for: 2 -> 0; matrix products, arithmetic and copies ran while one was open for 30% -> 0% of each run, Pallas kernels for 0% -> 0%
where the time goes in v1:
time: 282 us
  Pallas kernels  282 us (100%)
    pallas_call x1, Pallas kernels, on_device(): pl.pallas_call(functools.partial(gather_kernel, prows, pcols), out_shape=...  227 us
    pallas_call x1, Pallas kernels, on_device(): pl.pallas_call(functools.partial(update_kernel, prows, pcols), out_shape=...  54.4 us

profile of v1, /device:TPU:25, one launch (start us, length us, event | category | flops | bytes accessed | tf_op | source)
XLA Modules:
  0.0 281.5 jit_solution(3804925541414446354)
XLA Ops:
  0.0 227.1 %gather.1 = (f32[16,4,256,256]{3,2,1,0:T(8,128)}, f32[8,4,256,256]{3,2,1,0:T(8,128)}, f32[16,256,256]{2,1,0:T(8,128)}) custom-call(f32[16,1,256,8,1,256]{5,4,3,2,1,0:T(1,128)} %matrix.3, f32[16,1,256,8,1,256]{5,4,3,2,1,0:T(1,128)} %factor.1), custom_call_target="tpu_custom_call" | custom-call | tf_op jit(solution)/shard_map/gather/pallas_call | solution.py:486
  227.1 54.4 %update.1 = f32[16,1,256,8,1,256]{5,4,3,2,1,0:T(1,128)} custom-call(f32[16,1,256,8,1,256]{5,4,3,2,1,0:T(1,128)} %matrix.3, f32[16,4,256,256]{3,2,1,0:T(8,128)} %get-tuple-element.8.row_in, f32[8,4,256,256]{3,2,1,0:T(8,128)} %get-tuple-element.9.col_in, f32[16,256,256]{2,1,0:T(8,128)} %get-tuple-element.10.fin_in), custom_call_target="tpu_custom_call" | custom-call | tf_op jit(solution)/shard_map/update/pallas_call | solution.py:517

commit v2 on v1

v2 whole, which is shorter than its diff:
```python
import functools

import jax
import jax.numpy as jnp
from jax import lax
from jax.experimental import pallas as pl
from jax.experimental.pallas import tpu as pltpu
from jax.sharding import PartitionSpec as P

MESH = pl.DeviceIdType.MESH
CORES = 2
NEAR = 2
FAR = 3
SENT = 4
EARLY_NEAR = 3
EARLY_FAR = 6
PARTS = 4
LIMIT = 60 * 1024 * 1024

highest = lax.Precision.HIGHEST


def dot(left, right):
    return jnp.dot(left, right, precision=highest, preferred_element_type=jnp.float32)


def dot_trans(left, right, precision=highest):
    return lax.dot_general(
        left, right, (((1,), (1,)), ((), ())), precision=precision, preferred_element_type=jnp.float32
    )


def grid_of(count):
    across = 1
    while across * across * 4 <= count:
        across *= 2
    return count // across, across


def lanes_of(prows):
    return 2 if max(grid_of(prows)) <= 2 else 4


def early_pairs(row_tiles):
    return max(1, row_tiles // 2 * 7 // 8)


def pair_columns(pair, ratio):
    return (2 * pair + 1) // ratio + 1


def split(value):
    high = value.astype(jnp.bfloat16)
    return high, (value - high.astype(jnp.float32)).astype(jnp.bfloat16)


def split_rows(first, second, row_high, row_low):
    width = first.shape[-1]
    for place, tiles in enumerate((first, second)):
        for kind in range(4):
            upper, lower = split(tiles[kind])
            row_high[place * width:(place + 1) * width, kind * width:(kind + 1) * width] = upper
            row_low[place * width:(place + 1) * width, kind * width:(kind + 1) * width] = lower


def split_column(tiles, high, low):
    width = tiles.shape[-1]
    for kind in range(4):
        upper, lower = split(tiles[kind])
        place = (kind + 2) % 4 * width
        high[:, place:place + width] = upper
        low[:, place:place + width] = lower


def subtract_update(tiles, row_high, row_low, high, low, row_tile, prows, col_tile):
    width = tiles.shape[-1]
    total = (
        dot_trans(row_high[...], low[...], None)
        + dot_trans(row_low[...], high[...], None)
        + dot_trans(row_high[...], high[...], None)
    )
    row_id = lax.broadcasted_iota(jnp.int32, (width, width), 0)
    col_id = lax.broadcasted_iota(jnp.int32, (width, width), 1)
    for place in range(2):
        gap = (row_tile + place * prows - col_tile) * width
        part = total[place * width:(place + 1) * width]
        tiles[place] = tiles[place] - jnp.where(row_id + gap >= col_id, part, 0.0)


def gather_kernel(
    prows, pcols, matrix, factor, row_out, high_out, low_out, fin_out, done_out,
    rows, cols, panel, corner, inverse, core, half, row_high, row_low, col_high, col_low, tiles,
    load_sem, down_recv, side_recv, col_recv, col_fine, corner_recv, corner_send,
    down_send, side_send, col_send, send_fine, relay_send, relay_fine, out_sem, row_sem, column_sem, tile_load, tile_out,
):
    row_tiles, _, width, _ = rows.shape
    col_tiles = cols.shape[0]
    high, across = grid_of(prows)
    depth = pcols // CORES
    ratio = pcols // prows
    prow = lax.axis_index("prow")
    pcol = lax.axis_index("pcol")
    plane = pcol // CORES
    side = pcol % CORES
    y, x = prow // across, prow % across
    top = plane == 0

    barrier = pltpu.get_barrier_semaphore()

    def greet(where):
        pl.semaphore_signal(barrier, inc=1, device_id=where, device_id_type=MESH)

    def greet_plane(index, _):
        other = (index // CORES, plane * CORES + index % CORES)

        @pl.when(index != prow * CORES + side)
        def _():
            greet(other)

        return 0

    lax.fori_loop(0, prows * CORES, greet_plane, 0)

    @pl.when(plane > 0)
    def _():
        greet((prow, pcol - CORES))

    @pl.when(plane < depth - 1)
    def _():
        greet((prow, pcol + CORES))

    greeted = prows * CORES - 1 + jnp.where(plane > 0, 1, 0) + jnp.where(plane < depth - 1, 1, 0)
    pl.semaphore_wait(barrier, greeted)

    def remote(source, target, send, recv, where):
        return pltpu.make_async_remote_copy(
            src_ref=source, dst_ref=target, send_sem=send, recv_sem=recv, device_id=where, device_id_type=MESH
        )

    chunk = width // PARTS
    lanes = lanes_of(prows)
    work_lag = 3 if ratio > 1 else 5

    def span(part):
        return pl.ds(pl.multiple_of(part * chunk, chunk), chunk)

    def by_parts(i, late, part, whole, piece):
        fine = (i >= row_tiles - ratio) & (late == 1)

        @pl.when(fine)
        def _():
            piece()

        @pl.when(jnp.logical_not(fine) & (part == PARTS - 1))
        def _():
            whole()

    def down_copy(i, late, part):
        piece = rows.at[i, side + CORES * late, span(part)]
        return remote(
            piece, piece, down_send.at[i, late], down_recv.at[i, late, part], (prow, pcol + CORES)
        )

    def side_copy(i, late, kind):
        return remote(
            rows.at[i, kind], rows.at[i, kind], side_send.at[i, late], side_recv.at[i, late],
            (prow, plane * CORES + 1 - side),
        )

    def ways(source):
        ys, xs = source // across, source % across
        return (
            ((x == xs) & (y >= ys) & (y + 1 < high), prow + across),
            ((x == xs) & (y <= ys) & (y >= 1), prow - across),
            ((x >= xs) & (x + 1 < across), prow + 1),
            ((x <= xs) & (x >= 1), prow - 1),
        )

    def for_columns(i, late, part, act):
        kind = side + CORES * late
        for other in range(CORES):
            column = plane * CORES + other
            first = column // prows
            j = (i - first) // ratio

            @pl.when((column % prows == prow) & (i >= first) & ((i - first) % ratio == 0))
            def _():
                for way, (fits, where) in enumerate(ways(prow)):
                    @pl.when(fits)
                    def _():
                        lane = way * lanes // 4
                        by_parts(
                            i, late, part,
                            lambda: act(remote(
                                rows.at[i, kind], cols.at[j, kind], col_send.at[lane, j, late],
                                col_recv.at[j, kind], (where, column),
                            )),
                            lambda: act(remote(
                                rows.at[i, kind, span(part)], cols.at[j, kind, span(part)],
                                send_fine.at[lane, part], col_fine.at[side, part], (where, column),
                            )),
                        )

    def pass_down(i, late, part):
        @pl.when(jnp.logical_not(top))
        def _():
            down_copy(i, late, part).wait_recv()

        @pl.when(plane < depth - 1)
        def _():
            down_copy(i, late, part).start()

        @pl.when((part == PARTS - 1) | ((i >= row_tiles - ratio) & (late == 1)))
        def _():
            for_columns(i, late, part, lambda copy: copy.start())

    def pass_whole(i, late):
        def body(part, _):
            pass_down(i, late, part)
            return 0
        lax.fori_loop(0, PARTS, body, 0)

    def emit(i, late):
        side_copy(i, late, side + CORES * late).start()

    source = pcol % prows
    first_tile = pcol // prows
    far = (x != source % across) & (y != source // across)
    lag = jnp.where(far, FAR, NEAR)
    bridge = (x == source % across) & (y != source // across)
    early_lag = jnp.where(far, min(EARLY_FAR, row_tiles), min(EARLY_NEAR, row_tiles))

    def for_relay(i, late, act):
        j = (i - first_tile) // ratio

        @pl.when((prow != source) & (i >= first_tile) & (i < row_tiles) & ((i - first_tile) % ratio == 0))
        def _():
            def body(part, _):
                for kind in (CORES * late, CORES * late + 1):
                    by_parts(
                        i, late, part,
                        lambda: act(kind, cols.at[j, kind], relay_send.at[:, j, kind], col_recv.at[j, kind]),
                        lambda: act(
                            kind, cols.at[j, kind, span(part)],
                            relay_fine.at[:, kind % CORES, part], col_fine.at[kind % CORES, part],
                        ),
                    )
                return 0
            lax.fori_loop(0, PARTS, body, 0)

    def relay_copies(piece, send, recv, act):
        for way, (fits, where) in enumerate(ways(source)):
            @pl.when(fits)
            def _():
                act(remote(
                    piece, piece, send.at[way * lanes // 4], recv, (where, pcol),
                ))

    def arrive_column(kind, piece, send, recv):
        remote(piece, piece, send.at[0], recv, (prow, pcol)).wait_recv()
        relay_copies(piece, send, recv, lambda copy: copy.start())

    def relay(i, late):
        for_relay(i, late, arrive_column)

    def load(which, i):
        if which == 0:
            return pltpu.make_async_copy(factor.at[i, 0, :, 0, 0, :], rows.at[i, side], load_sem.at[0, i])
        return pltpu.make_async_copy(matrix.at[i, 0, :, 0, 0, :], panel.at[i], load_sem.at[1, i])

    owner = top & (prow < 2) & (side <= prow)
    slot = 2 * (prow + side)

    def corner_copy(which, index):
        sent = panel.at[0] if which == 0 else rows.at[0, side]
        return remote(
            sent, corner.at[slot + which], corner_send.at[which, index], corner_recv.at[slot + which],
            (index // CORES, index % CORES),
        )

    def each_peer(act):
        def body(index, _):
            @pl.when(index != prow * CORES + side)
            def _():
                for which in range(2):
                    act(corner_copy(which, index))
            return 0
        lax.fori_loop(0, prows * CORES, body, 0)

    row_id = lax.broadcasted_iota(jnp.int32, (width, width), 0)
    col_id = lax.broadcasted_iota(jnp.int32, (width, width), 1)

    @pl.when(top)
    def _():
        def start_loads(i, _):
            load(1, i).start()
            load(0, i).start()
            return 0
        lax.fori_loop(0, row_tiles, start_loads, 0)
        load(1, 0).wait()
        load(0, 0).wait()

        @pl.when(owner)
        def _():
            each_peer(lambda copy: copy.start())
            corner[slot] = panel[0]
            corner[slot + 1] = rows[0, side]

        pass_whole(0, 0)
        emit(0, 0)

        def send_early(i, _):
            load(0, i).wait()
            pass_whole(i, 0)
            emit(i, 0)
            return 0
        lax.fori_loop(1, row_tiles, send_early, 0)

        def await_corner(index, _):
            @pl.when(jnp.logical_not(owner & ((index == slot) | (index == slot + 1))))
            def _():
                remote(
                    corner.at[index], corner.at[index], corner_send.at[0, 0], corner_recv.at[index], (prow, pcol)
                ).wait_recv()
            return 0
        lax.fori_loop(0, 6, await_corner, 0)

        levels = (width - 1).bit_length()

        def invert(step, _):
            lower = corner[1 + 4 * step]
            diagonal = row_id == col_id
            inverse[step] = jnp.where(diagonal, 1.0 / jnp.where(diagonal, lower, 1.0), 0.0)

            def level(bit, _):
                block = lax.shift_right_logical(row_id, bit)
                under = (block % 2 == 1) & (lax.shift_right_logical(col_id, bit) == block - 1)
                now = inverse[step]
                cross = jnp.where(under, corner[1 + 4 * step], 0.0)
                inverse[step] = now - dot(dot(now, cross), now)
                return 0
            lax.fori_loop(0, levels, level, 0)
            return 0
        lax.fori_loop(0, 2, invert, 0)

        def core_of(block, inv):
            symmetric = block + block.T - jnp.where(row_id == col_id, block, 0.0)
            inner = dot_trans(dot(inv, symmetric), inv)
            return 0.5 * (inner + inner.T)

        core[0] = core_of(corner[0], inverse[0])
        half[...] = dot_trans(corner[2], inverse[0]) - 0.5 * dot(corner[3], core[0])
        cross = dot_trans(half[...], corner[3]) + dot_trans(corner[3], half[...])
        corner[4] = corner[4] - jnp.where(row_id >= col_id, cross, 0.0)
        core[1] = core_of(corner[4], inverse[1])

        @pl.when(owner)
        def _():
            each_peer(lambda copy: copy.wait_send())

    @pl.when(jnp.logical_not(top))
    def _():
        def pass_early(i, _):
            pass_whole(i, 0)
            emit(i, 0)
            relay(i - early_lag, 0)
            return 0
        lax.fori_loop(0, row_tiles, pass_early, 0)

    def reduce_tile(i):
        @pl.when(i > 0)
        def _():
            load(1, i).wait()

        @pl.when(side == 1)
        def _():
            for late in range(2):
                side_copy(i, late, 2 * late).wait_recv()
            panel[i] = (
                panel[i] - dot_trans(rows[i, 2], corner[3]) - dot_trans(rows[i, 0], half[...])
            )

        shared = dot(rows[i, side], core[side])
        halfway = dot_trans(panel[i], inverse[side]) - 0.5 * shared
        rows[i, side + 2] = halfway
        tile = i * prows + prow
        lower = jnp.where(row_id >= col_id, core[side], 0.0)
        final = halfway - 0.5 * shared
        final = jnp.where(tile > side, final, jnp.where(tile == side, lower, 0.0))
        panel[i] = final

    early = early_pairs(row_tiles)

    def row_ready(i):
        @pl.when(jnp.logical_not(top & (side == 1)))
        def _():
            for late in range(2):
                side_copy(i, late, 1 - side + 2 * late).wait_recv()

        @pl.when(i >= 2 * early)
        def _():
            pltpu.make_async_copy(rows.at[i], row_out.at[i - 2 * early], row_sem.at[i]).start()

    def column_out(j):
        return (
            pltpu.make_async_copy(col_high.at[j], high_out.at[j], column_sem.at[0, j]),
            pltpu.make_async_copy(col_low.at[j], low_out.at[j], column_sem.at[1, j]),
        )

    def column_ready(i):
        j = (i - first_tile) // ratio

        @pl.when((i >= first_tile) & (i < row_tiles) & ((i - first_tile) % ratio == 0))
        def _():
            @pl.when(prow == source)
            def _():
                split_column(rows.at[i], col_high.at[j], col_low.at[j])

            @pl.when(prow != source)
            def _():
                split_column(cols.at[j], col_high.at[j], col_low.at[j])

            @pl.when(j >= 1)
            def _():
                for copy in column_out(j - 1):
                    copy.start()

    def each_tile(pair, act):
        def body(j, _):
            for place in range(2):
                act(j, place)
            return 0
        lax.fori_loop(0, pair_columns(pair, ratio), body, 0)

    def tile_in(pair, j, place):
        return pltpu.make_async_copy(
            matrix.at[2 * pair + place, 0, :, j, 0, :], tiles.at[pair % 2, j, place], tile_load.at[pair % 2, j, place]
        )

    def tile_done(pair, j, place):
        return pltpu.make_async_copy(
            tiles.at[pair % 2, j, place], done_out.at[pair, j, place], tile_out.at[pair % 2, j, place]
        )

    def work(i, part):
        step = i - 1 - work_lag
        pair = step // 2
        slot = step % 2 * PARTS + part
        last = pair_columns(pair, ratio) - 1
        j = jnp.where(slot == 2 * PARTS - 1, last, slot)

        @pl.when((step >= 0) & (pair < early))
        def _():
            @pl.when(slot == 0)
            def _():
                @pl.when(pair >= 1)
                def _():
                    each_tile(pair - 1, lambda j, place: tile_done(pair - 1, j, place).wait())

                @pl.when(pair + 1 < early)
                def _():
                    each_tile(pair + 1, lambda j, place: tile_in(pair + 1, j, place).start())
                split_rows(rows.at[2 * pair], rows.at[2 * pair + 1], row_high, row_low)

            @pl.when((slot < last) | (slot == 2 * PARTS - 1))
            def _():
                for place in range(2):
                    tile_in(pair, j, place).wait()

                @pl.when((pcol >= 2) | (j > 0))
                def _():
                    subtract_update(
                        tiles.at[pair % 2, j], row_high, row_low, col_high.at[j], col_low.at[j],
                        2 * pair * prows + prow, prows, j * pcols + pcol,
                    )
                for place in range(2):
                    tile_done(pair, j, place).start()

    each_tile(0, lambda j, place: tile_in(0, j, place).start())

    @pl.when(top)
    def _():
        def reduce_step(i, _):
            @pl.when(i < row_tiles)
            def _():
                reduce_tile(i)

            @pl.when(i >= 1)
            def _():
                pass_whole(i - 1, 1)
                emit(i - 1, 1)
            return 0
        lax.fori_loop(0, row_tiles + 1, reduce_step, 0)

    def late_column(tile):
        relay(tile, 1)
        column_ready(tile)

    def drain(i, late):
        @pl.when(plane < depth - 1)
        def _():
            whole = rows.at[i, side + CORES * late]
            remote(whole, whole, down_send.at[i, late], down_recv.at[i, late, 0], (prow, pcol + CORES)).wait_send()

        if late:
            @pl.when(i >= row_tiles - ratio)
            def _():
                for part in range(PARTS - 1):
                    for_columns(i, late, part, lambda copy: copy.wait_send())
        for_columns(i, late, PARTS - 1, lambda copy: copy.wait_send())
        side_copy(i, late, side + 2 * late).wait_send()
        for_relay(
            i, late,
            lambda kind, piece, send, recv: relay_copies(piece, send, recv, lambda copy: copy.wait_send()),
        )

    def last_column(tile, _):
        late_column(tile)
        return 0

    def late_step(i, _):
        here = jnp.logical_not(top) & (i >= 1) & (i <= row_tiles)

        @pl.when(top & (i < row_tiles))
        def _():
            relay(i, 0)

        @pl.when(jnp.logical_not(top) & (i < early_lag))
        def _():
            relay(row_tiles - early_lag + i, 0)

        @pl.when(bridge & (i == row_tiles + 1))
        def _():
            lax.fori_loop(row_tiles - NEAR, row_tiles, last_column, 0)

        def part_step(part, _):
            @pl.when(here)
            def _():
                pass_down(i - 1, 1, part)

                @pl.when(part == PARTS - 1)
                def _():
                    emit(i - 1, 1)

            @pl.when((part == PARTS - 1) & jnp.logical_not(bridge & (i > row_tiles)))
            def _():
                late_column(i - 1 - lag)
            work(i, part)
            return 0
        lax.fori_loop(0, PARTS, part_step, 0)

        @pl.when((i >= 2) & (i < row_tiles + 2))
        def _():
            row_ready(i - 2)

        @pl.when(i < row_tiles)
        def _():
            drain(i, 0)

        @pl.when((i >= SENT) & (i < row_tiles + SENT))
        def _():
            drain(i - SENT, 1)
        return 0
    steps = max(row_tiles + 2, 2 * early + work_lag + 1)
    lax.fori_loop(0, steps, late_step, 0)

    @pl.when(jnp.logical_not(bridge))
    def _():
        lax.fori_loop(steps - 1 - lag, row_tiles, last_column, 0)
    for copy in column_out(col_tiles - 1):
        copy.start()
    each_tile(early - 1, lambda j, place: tile_done(early - 1, j, place).wait())

    fin_copy = pltpu.make_async_copy(panel, fin_out, out_sem)

    @pl.when(top)
    def _():
        fin_copy.start()

    def drain_rest(i, _):
        drain(i, 1)
        return 0
    lax.fori_loop(max(0, steps - SENT), row_tiles, drain_rest, 0)

    def drain_out(i, _):
        @pl.when(i >= 2 * early)
        def _():
            pltpu.make_async_copy(rows.at[i], row_out.at[i - 2 * early], row_sem.at[i]).wait()
        return 0
    lax.fori_loop(0, row_tiles, drain_out, 0)

    def drain_column(j, _):
        for copy in column_out(j):
            copy.wait()
        return 0
    lax.fori_loop(0, col_tiles, drain_column, 0)

    @pl.when(top)
    def _():
        fin_copy.wait()


def update_kernel(
    prows, pcols, matrix, row_in, high_in, low_in, fin_in, done_in, out,
    rows, row_high, row_low, col_high, col_low, tiles, zeros,
    row_sem, col_sem, in_sem, out_sem,
):
    row_tiles, col_tiles, width, _ = tiles.shape
    ratio = pcols // prows
    early = early_pairs(row_tiles)
    pairs = row_tiles // 2
    prow = lax.axis_index("prow")
    pcol = lax.axis_index("pcol")
    zeros[...] = jnp.zeros_like(zeros)

    def col_copies(j):
        return (
            pltpu.make_async_copy(high_in.at[j], col_high.at[j], col_sem.at[0, j]),
            pltpu.make_async_copy(low_in.at[j], col_low.at[j], col_sem.at[1, j]),
        )

    def row_copy(i):
        return pltpu.make_async_copy(row_in.at[i], rows.at[i], row_sem.at[i])

    def live(i, j):
        return j * pcols + pcol <= i * prows + prow

    def is_fixed(j):
        return (pcol < 2) & (j == 0)

    def start_in(i, j):
        @pl.when(live(i, j))
        def _():
            @pl.when(is_fixed(j))
            def _():
                pltpu.make_async_copy(fin_in.at[i], tiles.at[i, j], in_sem.at[i, j]).start()

            @pl.when(jnp.logical_not(is_fixed(j)) & (i < 2 * early))
            def _():
                pltpu.make_async_copy(done_in.at[i // 2, j, i % 2], tiles.at[i, j], in_sem.at[i, j]).start()

            @pl.when(jnp.logical_not(is_fixed(j)) & (i >= 2 * early))
            def _():
                pltpu.make_async_copy(matrix.at[i, 0, :, j, 0, :], tiles.at[i, j], in_sem.at[i, j]).start()

    def wait_in(i, j):
        @pl.when(live(i, j))
        def _():
            pltpu.make_async_copy(fin_in.at[i], tiles.at[i, j], in_sem.at[i, j]).wait()

    def out_copy(i, j):
        return pltpu.make_async_copy(tiles.at[i, j], out.at[i, 0, :, j, 0, :], out_sem.at[i, j])

    def start_out(i, j):
        @pl.when(live(i, j))
        def _():
            out_copy(i, j).start()

    def over_columns(i, count, act):
        def body(j, _):
            act(i, j)
            return 0
        lax.fori_loop(0, count, body, 0)

    def load_row(i, _):
        over_columns(i, col_tiles, start_in)
        return 0

    def zero_row(i):
        def body(j, _):
            @pl.when(jnp.logical_not(live(i, j)))
            def _():
                pltpu.make_async_copy(zeros, out.at[i, 0, :, j, 0, :], out_sem.at[i, j]).start()
            return 0
        lax.fori_loop(0, col_tiles, body, 0)

    for i in range(2):
        row_copy(i).start()
    for copy in col_copies(0):
        copy.start()
    lax.fori_loop(2 * early, 2 * early + 2, load_row, 0)
    for j in range(1, col_tiles):
        for copy in col_copies(j):
            copy.start()
    for i in range(2, row_tiles - 2 * early):
        row_copy(i).start()
    lax.fori_loop(2 * early + 2, row_tiles, load_row, 0)

    def feed(step):
        for place in range(2):
            i = 2 * step + place

            @pl.when(i < row_tiles)
            def _():
                @pl.when(i < 2 * early)
                def _():
                    load_row(i, 0)
                zero_row(i)

    def hand_on(i):
        @pl.when((i >= 0) & (i < 2 * early))
        def _():
            over_columns(i, col_tiles, wait_in)
            over_columns(i, col_tiles, start_out)

    def hand_pair(step):
        for place in range(2):
            hand_on(2 * step + place)

    def pair_step(pair, passed):
        for place in range(2):
            row_copy(2 * (pair - early) + place).wait()
        split_rows(
            rows.at[2 * (pair - early)], rows.at[2 * (pair - early) + 1], row_high, row_low
        )
        count = pair_columns(pair, ratio)
        old = jnp.where(pair == early, 0, pair_columns(pair - 1, ratio))

        def tile_step(j, _):
            feed(passed + j)

            @pl.when(j >= old)
            def _():
                for copy in col_copies(j):
                    copy.wait()
            for place in range(2):
                wait_in(2 * pair + place, j)

            @pl.when(jnp.logical_not(is_fixed(j)))
            def _():
                subtract_update(
                    tiles.at[pl.ds(2 * pair, 2), j], row_high, row_low, col_high.at[j], col_low.at[j],
                    2 * pair * prows + prow, prows, j * pcols + pcol,
                )
            for place in range(2):
                start_out(2 * pair + place, j)
            hand_pair(passed + j - 2)
            return 0
        lax.fori_loop(0, count, tile_step, 0)
        return passed + count
    passed = lax.fori_loop(early, pairs, pair_step, 0)

    def feed_rest(step, _):
        feed(step)
        return 0
    lax.fori_loop(passed, pairs, feed_rest, 0)

    def hand_rest(step, _):
        hand_pair(step)
        return 0
    lax.fori_loop(jnp.maximum(passed - 2, 0), pairs, hand_rest, 0)

    def finish(i, _):
        def body(j, _):
            out_copy(i, j).wait()
            return 0
        lax.fori_loop(0, col_tiles, body, 0)
        return 0
    lax.fori_loop(0, row_tiles, finish, 0)


def on_device(matrix, factor):
    row_tiles, _, width, col_tiles, _, _ = matrix.shape
    prows = lax.axis_size("prow")
    pcols = lax.axis_size("pcol")
    tile = (width, width)
    f32 = jnp.float32
    anywhere = pl.BlockSpec(memory_space=pl.ANY)
    dma = pltpu.SemaphoreType.DMA
    early = early_pairs(row_tiles)
    reach = pair_columns(early - 1, pcols // prows)
    late_rows = row_tiles - 2 * early
    bf16 = jnp.bfloat16
    lanes = lanes_of(prows)
    row_all, high_all, low_all, fin, done = pl.pallas_call(
        functools.partial(gather_kernel, prows, pcols),
        out_shape=(
            jax.ShapeDtypeStruct((late_rows, 4) + tile, f32),
            jax.ShapeDtypeStruct((col_tiles, width, 4 * width), bf16),
            jax.ShapeDtypeStruct((col_tiles, width, 4 * width), bf16),
            jax.ShapeDtypeStruct((row_tiles,) + tile, f32),
            jax.ShapeDtypeStruct((early, reach, 2) + tile, f32),
        ),
        in_specs=[anywhere, anywhere],
        out_specs=(anywhere,) * 5,
        scratch_shapes=[
            pltpu.VMEM((row_tiles, 4) + tile, f32),
            pltpu.VMEM((col_tiles, 4) + tile, f32),
            pltpu.VMEM((row_tiles,) + tile, f32),
            pltpu.VMEM((6,) + tile, f32),
            pltpu.VMEM((2,) + tile, f32),
            pltpu.VMEM((2,) + tile, f32),
            pltpu.VMEM(tile, f32),
            pltpu.VMEM((2 * width, 4 * width), bf16),
            pltpu.VMEM((2 * width, 4 * width), bf16),
            pltpu.VMEM((col_tiles, width, 4 * width), bf16),
            pltpu.VMEM((col_tiles, width, 4 * width), bf16),
            pltpu.VMEM((2, reach, 2) + tile, f32),
            dma((2, row_tiles)),
            dma((row_tiles, 2, PARTS)),
            dma((row_tiles, 2)),
            dma((col_tiles, 4)),
            dma((2, PARTS)),
            dma((6,)),
            dma((2, prows * CORES)),
            dma((row_tiles, 2)),
            dma((row_tiles, 2)),
            dma((lanes, col_tiles, 2)),
            dma((lanes, PARTS)),
            dma((lanes, col_tiles, 4)),
            dma((lanes, 2, PARTS)),
            dma,
            dma((row_tiles,)),
            dma((2, col_tiles)),
            dma((2, reach, 2)),
            dma((2, reach, 2)),
        ],
        compiler_params=pltpu.CompilerParams(collective_id=0, has_side_effects=True, vmem_limit_bytes=LIMIT),
        name="gather",
    )(matrix, factor)
    return pl.pallas_call(
        functools.partial(update_kernel, prows, pcols),
        out_shape=jax.ShapeDtypeStruct(matrix.shape, f32),
        in_specs=[anywhere] * 6,
        out_specs=anywhere,
        scratch_shapes=[
            pltpu.VMEM((late_rows, 4) + tile, f32),
            pltpu.VMEM((2 * width, 4 * width), bf16),
            pltpu.VMEM((2 * width, 4 * width), bf16),
            pltpu.VMEM((col_tiles, width, 4 * width), bf16),
            pltpu.VMEM((col_tiles, width, 4 * width), bf16),
            pltpu.VMEM((row_tiles, col_tiles) + tile, f32),
            pltpu.VMEM(tile, f32),
            dma((late_rows,)),
            dma((2, col_tiles)),
            dma((row_tiles, col_tiles)),
            dma((row_tiles, col_tiles)),
        ],
        compiler_params=pltpu.CompilerParams(vmem_limit_bytes=LIMIT),
        name="update",
    )(matrix, row_all, high_all, low_all, fin, done)


def solution(mesh):
    placed = P(None, "prow", None, None, "pcol", None)
    return jax.shard_map(on_device, mesh=mesh, in_specs=(placed, placed), out_specs=placed, check_vma=False)
```

time: 282 us -> 236 us (0.84)
  Pallas kernels: 282 us -> 234 us
    pallas_call x1, Pallas kernels: 54.4 us -> 22.7 us  [on_device(): pl.pallas_call(functools.partial(update_kernel, prows, pcols), out_shape=...]
    pallas_call x1, Pallas kernels: 227 us -> 211 us  [on_device(): pl.pallas_call(functools.partial(gather_kernel, prows, pcols), out_shape=...]
where the time goes in v2:
time: 236 us; the launch traced here: 234 us
  Pallas kernels  234 us (99%)
    pallas_call x1, Pallas kernels, on_device(): pl.pallas_call(functools.partial(gather_kernel, prows, pcols), out_shape=...  211 us
    pallas_call x1, Pallas kernels, on_device(): pl.pallas_call(functools.partial(update_kernel, prows, pcols), out_shape=...  22.7 us

profile of v2, /device:TPU:25, one launch (start us, length us, event | category | flops | bytes accessed | tf_op | source)
XLA Modules:
  0.0 233.8 jit_solution(7388294177671279285)
XLA Ops:
  0.0 211.0 %gather.1 = (f32[2,4,256,256]{3,2,1,0:T(8,128)}, bf16[8,256,1024]{2,1,0:T(8,128)(2,1)}, bf16[8,256,1024]{2,1,0:T(8,128)(2,1)}, f32[16,256,256]{2,1,0:T(8,128)}, f32[7,7,2,256,256]{4,3,2,1,0:T(8,128)}) custom-call(f32[16,1,256,8,1,256]{5,4,3,2,1,0:T(1,128)} %matrix.3, f32[16,1,256,8,1,256]{5,4,3,2,1,0:T(1,128)} %factor.1), custom_call_target="tpu_custom_call" | custom-call | tf_op jit(solution)/shard_map/gather/pallas_call | solution.py:775
  211.0 22.7 %update.1 = f32[16,1,256,8,1,256]{5,4,3,2,1,0:T(1,128)} custom-call(f32[16,1,256,8,1,256]{5,4,3,2,1,0:T(1,128)} %matrix.3, f32[2,4,256,256]{3,2,1,0:T(8,128)} %get-tuple-element.10.row_in, bf16[8,256,1024]{2,1,0:T(8,128)(2,1)} %get-tuple-element.11.high_in, bf16[8,256,1024]{2,1,0:T(8,128)(2,1)} %get-tuple-element.12.low_in, ...), custom_call_target="tpu_custom_call" | custom-call | tf_op jit(solution)/shard_map/update/pallas_call | solution.py:821
